TPU v7x, 32 devices: a whole 2x2x4 slice. The times are simulated.
32 devices in a mesh: sub: 8 (over z, y), slab: 4 (over x, core).
Axes of the slice: x: 2, y: 2, z: 4, core: 2. Of those that a mesh axis runs over, the one named last changes fastest.
Arguments:
- rhs: float32 [8, 64, 8, 512], P(None, 'sub', None, 'slab'), may hold values from -60 to 60, as said below
- perm: float32 [64, 8, 512], P('sub', None, 'slab'), may hold values from 0.1 to 10
- accum: float32 [64, 8, 512], P('sub', None, 'slab'), may hold values from 0.05 to 0.5
- counts: int32 [8], replicated, may hold values from 1 to 8, as said below
Outputs:
- solution: float32 [8, 64, 8, 512], P(None, 'sub', None, 'slab')
- residual: float32 [8, 64, 8, 512], P(None, 'sub', None, 'slab')
Inputs may be any that keep to these rules, and one draw needn't show every extreme that they name: `rhs`: pressure sources of the 8 systems; values on planes that are not live are never read. counts[i] live planes fill the first slots of subdomain i; some subdomain has 8.
All inputs are finite; a program needn't handle non-finite values.
Results may differ from a plain program's by a relative error of at most 0.00045.
Values sent between devices are 32-bit elements; how exact they have to be, the bound alone decides.
A program may use at most 64 MiB of HBM per device.

v0:
```python
import jax
import jax.numpy as jnp
from jax import lax
from jax.sharding import PartitionSpec as P

S = 8
ITERS = 4
DEG = 4
cheb_low = 0.05
cheb_high = 2.0


def with_halo(cells, sides, width):
    for axis, dim in sides:
        count = lax.axis_size(axis)
        ends = count - 1
        head = lax.slice_in_dim(cells, 0, width, axis=dim)
        tail = lax.slice_in_dim(cells, cells.shape[dim] - width, cells.shape[dim], axis=dim)
        cells = jnp.concatenate(
            [
                lax.ppermute(tail, axis, [(i, (i + 1) % count) for i in range(ends)]),
                cells,
                lax.ppermute(head, axis, [((i + 1) % count, i) for i in range(ends)]),
            ],
            axis=dim,
        )
    return cells


def neighbours(field, live, plane):
    first = field[:, 0]
    last = lax.dynamic_index_in_dim(field, live - 1, 1, keepdims=False)
    edges = with_halo(jnp.stack([first, last], axis=1), (("sub", 1),), 1)
    before = edges[:, 0:1]
    after = edges[:, 3:4]
    zero_plane = jnp.zeros_like(field[:, :1])
    up_inside = jnp.concatenate([field[:, 1:], zero_plane], axis=1)
    down_inside = jnp.concatenate([zero_plane, field[:, :-1]], axis=1)
    x_next = jnp.where(plane == live - 1, after, up_inside)
    x_prev = jnp.where(plane == 0, before, down_inside)
    zero_row = jnp.zeros_like(field[:, :, :1])
    y_next = jnp.concatenate([field[:, :, 1:], zero_row], axis=2)
    y_prev = jnp.concatenate([zero_row, field[:, :, :-1]], axis=2)
    padded = with_halo(field, (("slab", 3),), 1)
    z_next = padded[..., 2:]
    z_prev = padded[..., :-2]
    return (x_next, x_prev, y_next, y_prev, z_next, z_prev)


def product(left, right):
    return lax.dot_general(
        left.reshape(left.shape[0], -1),
        right.reshape(right.shape[0], -1),
        (((1,), (1,)), ((), ())),
        precision=lax.Precision.HIGHEST,
    )


def combine(coef, block):
    flat = jnp.dot(coef, block.reshape(block.shape[0], -1), precision=lax.Precision.HIGHEST)
    return flat.reshape(block.shape)


def lower_solve(factor, block):
    flat = jax.scipy.linalg.solve_triangular(factor, block.reshape(block.shape[0], -1), lower=True)
    return flat.reshape(block.shape)


def precondition(vector, operate, inv_diag):
    theta = 0.5 * (cheb_high + cheb_low)
    delta = 0.5 * (cheb_high - cheb_low)
    sigma = theta / delta
    remain = vector
    update = inv_diag * remain * (1.0 / theta)
    result = update
    rho = 1.0 / sigma
    for step in range(DEG - 1):
        remain = remain - operate(update)
        rho_next = 1.0 / (2.0 * sigma - rho)
        update = rho_next * rho * update + 2.0 * rho_next / delta * (inv_diag * remain)
        result = result + update
        rho = rho_next
    return result


def small_solve(coefs, lowers, lead):
    hess = jnp.zeros((ITERS * S, (ITERS + 1) * S), jnp.float32)
    for j in range(ITERS):
        for i in range(j + 1):
            hess = hess.at[j * S : (j + 1) * S, i * S : (i + 1) * S].set(coefs[j][i])
        hess = hess.at[j * S : (j + 1) * S, (j + 1) * S : (j + 2) * S].set(lowers[j])
    target = jnp.zeros((S, (ITERS + 1) * S), jnp.float32).at[:, :S].set(lead)
    normal = jnp.dot(hess, hess.T, precision=lax.Precision.HIGHEST)
    right = jnp.dot(hess, target.T, precision=lax.Precision.HIGHEST)
    factor = jnp.linalg.cholesky(normal)
    mix = jax.scipy.linalg.cho_solve((factor, True), right).T
    return (mix, hess, target)


def body(rhs, perm, accum, counts):
    live = counts[lax.axis_index("sub")]
    depth = rhs.shape[1]
    plane = lax.broadcasted_iota(jnp.int32, (1, depth, 1, 1), 1)
    mask = (plane < live).astype(jnp.float32)
    field_perm = perm[None]
    near = neighbours(field_perm, live, plane)
    conduct = []
    diag = accum[None]
    for other in near:
        weight = 2.0 * field_perm * other / (field_perm + other)
        conduct.append(weight)
        diag = diag + weight
    inv_diag = mask / diag

    def operate(field):
        beside = neighbours(field, live, plane)
        total = diag * field
        for weight, other in zip(conduct, beside):
            total = total - weight * other
        return mask * total

    start = rhs * mask
    lead = jnp.linalg.cholesky(lax.psum(product(start, start), ("sub", "slab")))
    basis = [lower_solve(lead, start)]
    coefs = []
    lowers = []
    for step in range(ITERS):
        direction = precondition(basis[step], operate, inv_diag)
        work = operate(direction)
        stacked, whole = lax.psum(
            (jnp.stack([product(work, basis[i]) for i in range(step + 1)]), product(work, work)),
            ("sub", "slab"),
        )
        found = [stacked[i] for i in range(step + 1)]
        block = whole
        for i in range(step + 1):
            work = work - combine(found[i], basis[i])
            block = block - jnp.dot(found[i], found[i].T, precision=lax.Precision.HIGHEST)
        lower = jnp.linalg.cholesky(block)
        basis.append(lower_solve(lower, work))
        coefs.append(found)
        lowers.append(lower)
    mix, hess, target = small_solve(coefs, lowers, lead)
    combo = combine(mix[:, :S], basis[0])
    for j in range(1, ITERS):
        combo = combo + combine(mix[:, j * S : (j + 1) * S], basis[j])
    solution = precondition(combo, operate, inv_diag)
    residual = start - operate(solution)
    return (solution, residual)


def solution(mesh):
    placed = (P(None, "sub", None, "slab"), P("sub", None, "slab"), P("sub", None, "slab"), P())
    return jax.shard_map(
        body,
        mesh=mesh,
        in_specs=placed,
        out_specs=(P(None, "sub", None, "slab"), P(None, "sub", None, "slab")),
        check_vma=False,
    )
```

profile of v0, /device:TPU:2, one launch (start us, length us, event | category | flops | bytes accessed | tf_op | source)
XLA Modules:
  0.0 579.4 jit_solution(9655729661371559790)
XLA Ops:
  3.5 3.6 collective-permute-start.2
  16.0 42.4 %psum.63 = f32[8,8]{0,1:T(8,128)S(1)} all-reduce(f32[8,8]{0,1:T(8,128)S(1)} %convolution_bitcast_fusion.13), channel_id=1, replica_groups=mesh['sub'=8,'slab'=4] {'sub','slab'}, use_global_device_ids=true, to_apply=%region_0.1 | all-reduce | flops 64 | bytes 512 | tf_op jit(solution)/shard_map/psum | solution.py:123
  66.3 3.6 collective-permute-start.6
  74.7 4.2 collective-permute-done.4
  81.5 3.6 collective-permute-start.10
  85.2 4.4 collective-permute-start.9
  91.2 4.2 collective-permute-done.8
  98.0 3.6 collective-permute-start.14
  106.6 4.2 collective-permute-done.12
  113.4 3.6 collective-permute-start.18
  117.1 4.2 collective-permute-start.17
  122.8 4.2 collective-permute-done.16
  128.8 39.8 %all-reduce.89 = (f32[8,8]{1,0:T(8,128)S(1)}, f32[8,8]{0,1:T(8,128)S(1)}) all-reduce(f32[8,8]{1,0:T(8,128)S(1)} %fusion.290, f32[8,8]{0,1:T(8,128)S(1)} %convolution_bitcast_fusion.12), channel_id=1, replica_groups=mesh['sub'=8,'slab'=4] {'sub','slab'}, use_global_device_ids=true, to_apply=%region_3.6 | all-reduce | flops 128 | bytes 1024 | tf_op jit(solution)/shard_map/psum | solution.py:130
  177.1 3.6 collective-permute-start.22
  192.1 3.6 collective-permute-start.26
  195.8 4.8 collective-permute-start.25
  202.2 4.2 collective-permute-done.24
  209.0 3.6 collective-permute-start.30
  217.1 4.2 collective-permute-done.28
  223.9 3.6 collective-permute-start.34
  227.6 3.9 collective-permute-start.33
  233.1 4.2 collective-permute-done.32
  239.8 39.4 %all-reduce.88 = (f32[2,8,8]{2,1,0:T(8,128)S(1)}, f32[8,8]{0,1:T(8,128)S(1)}) all-reduce(f32[2,8,8]{2,1,0:T(8,128)S(1)} %pad_maximum_fusion.44, f32[8,8]{0,1:T(8,128)S(1)} %convolution_bitcast_fusion.9), channel_id=1, replica_groups=mesh['sub'=8,'slab'=4] {'sub','slab'}, use_global_device_ids=true, to_apply=%region_6.9 | all-reduce | flops 192 | bytes 1536 | tf_op jit(solution)/shard_map/psum | solution.py:130
  286.4 3.6 collective-permute-start.38
  301.3 3.6 collective-permute-start.42
  305.0 4.8 collective-permute-start.41
  311.4 4.2 collective-permute-done.40
  318.2 3.6 collective-permute-start.46
  326.4 4.2 collective-permute-done.44
  333.2 3.6 collective-permute-start.50
  336.8 3.9 collective-permute-start.49
  342.3 4.2 collective-permute-done.48
  349.8 39.5 %all-reduce.87 = (f32[3,8,8]{2,1,0:T(8,128)S(1)}, f32[8,8]{0,1:T(8,128)S(1)}) all-reduce(f32[3,8,8]{2,1,0:T(8,128)S(1)} %pad_maximum_fusion.43, f32[8,8]{0,1:T(8,128)S(1)} %convolution_bitcast_fusion.5), channel_id=1, replica_groups=mesh['sub'=8,'slab'=4] {'sub','slab'}, use_global_device_ids=true, to_apply=%region_8.11 | all-reduce | flops 256 | bytes 2048 | tf_op jit(solution)/shard_map/psum | solution.py:130
  411.9 3.6 collective-permute-start.58
  415.6 4.8 collective-permute-start.57
  422.0 4.2 collective-permute-done.56
  428.8 3.6 collective-permute-start.62
  437.3 4.2 collective-permute-done.60
  444.2 3.6 collective-permute-start.66
  452.9 4.2 collective-permute-done.64
  461.1 39.9 %all-reduce.86 = (f32[4,8,8]{2,1,0:T(8,128)S(1)}, f32[8,8]{0,1:T(8,128)S(1)}) all-reduce(f32[4,8,8]{2,1,0:T(8,128)S(1)} %pad_maximum_fusion.42, f32[8,8]{0,1:T(8,128)S(1)} %convolution_bitcast_fusion), channel_id=1, replica_groups=mesh['sub'=8,'slab'=4] {'sub','slab'}, use_global_device_ids=true, to_apply=%region_10.13 | all-reduce | flops 320 | bytes 2560 | tf_op jit(solution)/shard_map/psum | solution.py:130
  517.5 3.6 collective-permute-start.70
  525.3 4.7 collective-permute-done.68
  536.3 4.8 collective-permute-start.73
  542.7 4.2 collective-permute-done.72
  557.5 4.2 collective-permute-done.76
  568.0 4.0 collective-permute-start.81
  574.1 3.7 collective-permute-done.80
  (363 shorter events, 200.5 us)
Async XLA Ops:
  1.6 61.9 %collective-permute-start.3 = (f32[1,8,8,1]{3,2,1,0:T(8,128)S(1)}, f32[1,8,8,1]{3,2,1,0:T(8,128)S(1)}, u32[]{:S(2)}, u32[]{:S(2)}) collective-permute-start(f32[1,8,8,1]{3,2,1,0:T(8,128)S(1)} %get-tuple-element.393), channel_id=1, source_target_pairs={{0,1},{1,2},{2,3},{4,5},{5,6},{6,7},{8,9},{9,10},{10,11},{12,13},{... | collective-permute-start | bytes 776 | tf_op jit(solution)/shard_map/ppermute | solution.py:21
  3.5 60.0 %collective-permute-start.2 = (f32[1,8,8,1]{3,2,1,0:T(8,128)S(1)}, f32[1,8,8,1]{3,2,1,0:T(8,128)S(1)}, u32[]{:S(2)}, u32[]{:S(2)}) collective-permute-start(f32[1,8,8,1]{3,2,1,0:T(8,128)S(1)} %get-tuple-element.392), channel_id=1, source_target_pairs={{1,0},{2,1},{3,2},{5,4},{6,5},{7,6},{9,8},{10,9},{11,10},{13,12},{... | collective-permute-start | bytes 776 | tf_op jit(solution)/shard_map/ppermute | solution.py:23
  9.1 54.4 %collective-permute-start.1 = (f32[1,1,8,128]{3,2,1,0:T(8,128)S(1)}, f32[1,1,8,128]{3,2,1,0:T(8,128)S(1)}, u32[]{:S(2)}, u32[]{:S(2)}) collective-permute-start(f32[1,1,8,128]{3,2,1,0:T(8,128)S(1)} %fusion.154), channel_id=1, source_target_pairs={{0,4},{4,8},{8,12},{12,16},{16,20},{20,24},{24,28},{1,5},{5,9},{9,... | collective-permute-start | bytes 12296 | tf_op jit(solution)/shard_map/ppermute | solution.py:21
  12.6 51.0 %collective-permute-start = (f32[1,1,8,128]{3,2,1,0:T(8,128)S(1)}, f32[1,1,8,128]{3,2,1,0:T(8,128)S(1)}, u32[]{:S(2)}, u32[]{:S(2)}) collective-permute-start(f32[1,1,8,128]{3,2,1,0:T(8,128)S(1)} %slice.1210), channel_id=1, source_target_pairs={{4,0},{8,4},{12,8},{16,12},{20,16},{24,20},{28,24},{5,1},{9,5},{13... | collective-permute-start | bytes 12296 | tf_op jit(solution)/shard_map/ppermute | solution.py:23
  64.3 10.3 %collective-permute-start.7 = (f32[8,8,8,1]{3,0,2,1:T(8,128)S(1)}, f32[8,8,8,1]{3,0,2,1:T(8,128)S(1)}, u32[]{:S(2)}, u32[]{:S(2)}) collective-permute-start(f32[8,8,8,1]{3,0,2,1:T(8,128)S(1)} %get-tuple-element.379), channel_id=1, source_target_pairs={{0,1},{1,2},{2,3},{4,5},{5,6},{6,7},{8,9},{9,10},{10,11},{12,13},{... | collective-permute-start | bytes 6152 | tf_op jit(solution)/shard_map/ppermute | solution.py:21
  66.3 8.4 %collective-permute-start.6 = (f32[8,8,8,1]{3,0,2,1:T(8,128)S(1)}, f32[8,8,8,1]{3,0,2,1:T(8,128)S(1)}, u32[]{:S(2)}, u32[]{:S(2)}) collective-permute-start(f32[8,8,8,1]{3,0,2,1:T(8,128)S(1)} %get-tuple-element.378), channel_id=1, source_target_pairs={{1,0},{2,1},{3,2},{5,4},{6,5},{7,6},{9,8},{10,9},{11,10},{13,12},{... | collective-permute-start | bytes 6152 | tf_op jit(solution)/shard_map/ppermute | solution.py:23
  79.6 11.4 %collective-permute-start.11 = (f32[8,8,8,1]{3,0,2,1:T(8,128)S(1)}, f32[8,8,8,1]{3,0,2,1:T(8,128)S(1)}, u32[]{:S(2)}, u32[]{:S(2)}) collective-permute-start(f32[8,8,8,1]{3,0,2,1:T(8,128)S(1)} %get-tuple-element.371), channel_id=1, source_target_pairs={{0,1},{1,2},{2,3},{4,5},{5,6},{6,7},{8,9},{9,10},{10,11},{12,13},{... | collective-permute-start | bytes 6152 | tf_op jit(solution)/shard_map/ppermute | solution.py:21
  81.5 9.4 %collective-permute-start.10 = (f32[8,8,8,1]{3,0,2,1:T(8,128)S(1)}, f32[8,8,8,1]{3,0,2,1:T(8,128)S(1)}, u32[]{:S(2)}, u32[]{:S(2)}) collective-permute-start(f32[8,8,8,1]{3,0,2,1:T(8,128)S(1)} %get-tuple-element.370), channel_id=1, source_target_pairs={{1,0},{2,1},{3,2},{5,4},{6,5},{7,6},{9,8},{10,9},{11,10},{13,12},{... | collective-permute-start | bytes 6152 | tf_op jit(solution)/shard_map/ppermute | solution.py:23
  96.0 10.3 %collective-permute-start.15 = (f32[8,8,8,1]{3,0,2,1:T(8,128)S(1)}, f32[8,8,8,1]{3,0,2,1:T(8,128)S(1)}, u32[]{:S(2)}, u32[]{:S(2)}) collective-permute-start(f32[8,8,8,1]{3,0,2,1:T(8,128)S(1)} %get-tuple-element.363), channel_id=1, source_target_pairs={{0,1},{1,2},{2,3},{4,5},{5,6},{6,7},{8,9},{9,10},{10,11},{12,13},{... | collective-permute-start | bytes 6152 | tf_op jit(solution)/shard_map/ppermute | solution.py:21
  98.0 8.4 %collective-permute-start.14 = (f32[8,8,8,1]{3,0,2,1:T(8,128)S(1)}, f32[8,8,8,1]{3,0,2,1:T(8,128)S(1)}, u32[]{:S(2)}, u32[]{:S(2)}) collective-permute-start(f32[8,8,8,1]{3,0,2,1:T(8,128)S(1)} %get-tuple-element.362), channel_id=1, source_target_pairs={{1,0},{2,1},{3,2},{5,4},{6,5},{7,6},{9,8},{10,9},{11,10},{13,12},{... | collective-permute-start | bytes 6152 | tf_op jit(solution)/shard_map/ppermute | solution.py:23
  111.5 11.1 %collective-permute-start.19 = (f32[8,8,8,1]{3,0,2,1:T(8,128)S(1)}, f32[8,8,8,1]{3,0,2,1:T(8,128)S(1)}, u32[]{:S(2)}, u32[]{:S(2)}) collective-permute-start(f32[8,8,8,1]{3,0,2,1:T(8,128)S(1)} %get-tuple-element.355), channel_id=1, source_target_pairs={{0,1},{1,2},{2,3},{4,5},{5,6},{6,7},{8,9},{9,10},{10,11},{12,13},{... | collective-permute-start | bytes 6152 | tf_op jit(solution)/shard_map/ppermute | solution.py:21
  113.4 9.2 %collective-permute-start.18 = (f32[8,8,8,1]{3,0,2,1:T(8,128)S(1)}, f32[8,8,8,1]{3,0,2,1:T(8,128)S(1)}, u32[]{:S(2)}, u32[]{:S(2)}) collective-permute-start(f32[8,8,8,1]{3,0,2,1:T(8,128)S(1)} %get-tuple-element.354), channel_id=1, source_target_pairs={{1,0},{2,1},{3,2},{5,4},{6,5},{7,6},{9,8},{10,9},{11,10},{13,12},{... | collective-permute-start | bytes 6152 | tf_op jit(solution)/shard_map/ppermute | solution.py:23
  175.2 11.4 %collective-permute-start.23 = (f32[8,8,8,1]{3,0,2,1:T(8,128)}, f32[8,8,8,1]{3,0,2,1:T(8,128)S(1)}, u32[]{:S(2)}, u32[]{:S(2)}) collective-permute-start(f32[8,8,8,1]{3,0,2,1:T(8,128)} %get-tuple-element.347), channel_id=1, source_target_pairs={{0,1},{1,2},{2,3},{4,5},{5,6},{6,7},{8,9},{9,10},{10,11},{12,13},{... | collective-permute-start | bytes 6152 | tf_op jit(solution)/shard_map/ppermute | solution.py:21
  177.1 9.4 %collective-permute-start.22 = (f32[8,8,8,1]{3,0,2,1:T(8,128)S(1)}, f32[8,8,8,1]{3,0,2,1:T(8,128)S(1)}, u32[]{:S(2)}, u32[]{:S(2)}) collective-permute-start(f32[8,8,8,1]{3,0,2,1:T(8,128)S(1)} %get-tuple-element.346), channel_id=1, source_target_pairs={{1,0},{2,1},{3,2},{5,4},{6,5},{7,6},{9,8},{10,9},{11,10},{13,12},{... | collective-permute-start | bytes 6152 | tf_op jit(solution)/shard_map/ppermute | solution.py:23
  190.2 11.8 %collective-permute-start.27 = (f32[8,8,8,1]{3,0,2,1:T(8,128)S(1)}, f32[8,8,8,1]{3,0,2,1:T(8,128)S(1)}, u32[]{:S(2)}, u32[]{:S(2)}) collective-permute-start(f32[8,8,8,1]{3,0,2,1:T(8,128)S(1)} %get-tuple-element.339), channel_id=1, source_target_pairs={{0,1},{1,2},{2,3},{4,5},{5,6},{6,7},{8,9},{9,10},{10,11},{12,13},{... | collective-permute-start | bytes 6152 | tf_op jit(solution)/shard_map/ppermute | solution.py:21
  192.1 9.8 %collective-permute-start.26 = (f32[8,8,8,1]{3,0,2,1:T(8,128)S(1)}, f32[8,8,8,1]{3,0,2,1:T(8,128)S(1)}, u32[]{:S(2)}, u32[]{:S(2)}) collective-permute-start(f32[8,8,8,1]{3,0,2,1:T(8,128)S(1)} %get-tuple-element.338), channel_id=1, source_target_pairs={{1,0},{2,1},{3,2},{5,4},{6,5},{7,6},{9,8},{10,9},{11,10},{13,12},{... | collective-permute-start | bytes 6152 | tf_op jit(solution)/shard_map/ppermute | solution.py:23
  195.8 6.4 %collective-permute-start.25 = (f32[8,1,8,128]{3,0,2,1:T(8,128)S(1)}, f32[8,1,8,128]{3,0,2,1:T(8,128)S(1)}, u32[]{:S(2)}, u32[]{:S(2)}) collective-permute-start(f32[8,1,8,128]{3,0,2,1:T(8,128)S(1)} %get-tuple-element.333), channel_id=1, source_target_pairs={{0,4},{4,8},{8,12},{12,16},{16,20},{20,24},{24,28},{1,5},{5,9},{9,... | collective-permute-start | bytes 98312 | tf_op jit(solution)/shard_map/ppermute | solution.py:21
  207.0 9.9 %collective-permute-start.31 = (f32[8,8,8,1]{3,0,2,1:T(8,128)S(1)}, f32[8,8,8,1]{3,0,2,1:T(8,128)S(1)}, u32[]{:S(2)}, u32[]{:S(2)}) collective-permute-start(f32[8,8,8,1]{3,0,2,1:T(8,128)S(1)} %get-tuple-element.331), channel_id=1, source_target_pairs={{0,1},{1,2},{2,3},{4,5},{5,6},{6,7},{8,9},{9,10},{10,11},{12,13},{... | collective-permute-start | bytes 6152 | tf_op jit(solution)/shard_map/ppermute | solution.py:21
  209.0 7.9 %collective-permute-start.30 = (f32[8,8,8,1]{3,0,2,1:T(8,128)S(1)}, f32[8,8,8,1]{3,0,2,1:T(8,128)S(1)}, u32[]{:S(2)}, u32[]{:S(2)}) collective-permute-start(f32[8,8,8,1]{3,0,2,1:T(8,128)S(1)} %get-tuple-element.330), channel_id=1, source_target_pairs={{1,0},{2,1},{3,2},{5,4},{6,5},{7,6},{9,8},{10,9},{11,10},{13,12},{... | collective-permute-start | bytes 6152 | tf_op jit(solution)/shard_map/ppermute | solution.py:23
  222.0 11.0 %collective-permute-start.35 = (f32[8,8,8,1]{3,0,2,1:T(8,128)S(1)}, f32[8,8,8,1]{3,0,2,1:T(8,128)S(1)}, u32[]{:S(2)}, u32[]{:S(2)}) collective-permute-start(f32[8,8,8,1]{3,0,2,1:T(8,128)S(1)} %get-tuple-element.323), channel_id=1, source_target_pairs={{0,1},{1,2},{2,3},{4,5},{5,6},{6,7},{8,9},{9,10},{10,11},{12,13},{... | collective-permute-start | bytes 6152 | tf_op jit(solution)/shard_map/ppermute | solution.py:21
  223.9 9.1 %collective-permute-start.34 = (f32[8,8,8,1]{3,0,2,1:T(8,128)S(1)}, f32[8,8,8,1]{3,0,2,1:T(8,128)S(1)}, u32[]{:S(2)}, u32[]{:S(2)}) collective-permute-start(f32[8,8,8,1]{3,0,2,1:T(8,128)S(1)} %get-tuple-element.322), channel_id=1, source_target_pairs={{1,0},{2,1},{3,2},{5,4},{6,5},{7,6},{9,8},{10,9},{11,10},{13,12},{... | collective-permute-start | bytes 6152 | tf_op jit(solution)/shard_map/ppermute | solution.py:23
  284.4 11.4 %collective-permute-start.39 = (f32[8,8,8,1]{3,0,2,1:T(8,128)}, f32[8,8,8,1]{3,0,2,1:T(8,128)S(1)}, u32[]{:S(2)}, u32[]{:S(2)}) collective-permute-start(f32[8,8,8,1]{3,0,2,1:T(8,128)} %get-tuple-element.315), channel_id=1, source_target_pairs={{0,1},{1,2},{2,3},{4,5},{5,6},{6,7},{8,9},{9,10},{10,11},{12,13},{... | collective-permute-start | bytes 6152 | tf_op jit(solution)/shard_map/ppermute | solution.py:21
  286.4 9.5 %collective-permute-start.38 = (f32[8,8,8,1]{3,0,2,1:T(8,128)S(1)}, f32[8,8,8,1]{3,0,2,1:T(8,128)S(1)}, u32[]{:S(2)}, u32[]{:S(2)}) collective-permute-start(f32[8,8,8,1]{3,0,2,1:T(8,128)S(1)} %get-tuple-element.314), channel_id=1, source_target_pairs={{1,0},{2,1},{3,2},{5,4},{6,5},{7,6},{9,8},{10,9},{11,10},{13,12},{... | collective-permute-start | bytes 6152 | tf_op jit(solution)/shard_map/ppermute | solution.py:23
  299.4 11.8 %collective-permute-start.43 = (f32[8,8,8,1]{3,0,2,1:T(8,128)S(1)}, f32[8,8,8,1]{3,0,2,1:T(8,128)S(1)}, u32[]{:S(2)}, u32[]{:S(2)}) collective-permute-start(f32[8,8,8,1]{3,0,2,1:T(8,128)S(1)} %get-tuple-element.307), channel_id=1, source_target_pairs={{0,1},{1,2},{2,3},{4,5},{5,6},{6,7},{8,9},{9,10},{10,11},{12,13},{... | collective-permute-start | bytes 6152 | tf_op jit(solution)/shard_map/ppermute | solution.py:21
  301.3 9.8 %collective-permute-start.42 = (f32[8,8,8,1]{3,0,2,1:T(8,128)S(1)}, f32[8,8,8,1]{3,0,2,1:T(8,128)S(1)}, u32[]{:S(2)}, u32[]{:S(2)}) collective-permute-start(f32[8,8,8,1]{3,0,2,1:T(8,128)S(1)} %get-tuple-element.306), channel_id=1, source_target_pairs={{1,0},{2,1},{3,2},{5,4},{6,5},{7,6},{9,8},{10,9},{11,10},{13,12},{... | collective-permute-start | bytes 6152 | tf_op jit(solution)/shard_map/ppermute | solution.py:23
  305.0 6.4 %collective-permute-start.41 = (f32[8,1,8,128]{3,0,2,1:T(8,128)S(1)}, f32[8,1,8,128]{3,0,2,1:T(8,128)S(1)}, u32[]{:S(2)}, u32[]{:S(2)}) collective-permute-start(f32[8,1,8,128]{3,0,2,1:T(8,128)S(1)} %get-tuple-element.301), channel_id=1, source_target_pairs={{0,4},{4,8},{8,12},{12,16},{16,20},{20,24},{24,28},{1,5},{5,9},{9,... | collective-permute-start | bytes 98312 | tf_op jit(solution)/shard_map/ppermute | solution.py:21
  316.3 9.9 %collective-permute-start.47 = (f32[8,8,8,1]{3,0,2,1:T(8,128)S(1)}, f32[8,8,8,1]{3,0,2,1:T(8,128)S(1)}, u32[]{:S(2)}, u32[]{:S(2)}) collective-permute-start(f32[8,8,8,1]{3,0,2,1:T(8,128)S(1)} %get-tuple-element.299), channel_id=1, source_target_pairs={{0,1},{1,2},{2,3},{4,5},{5,6},{6,7},{8,9},{9,10},{10,11},{12,13},{... | collective-permute-start | bytes 6152 | tf_op jit(solution)/shard_map/ppermute | solution.py:21
  318.2 8.0 %collective-permute-start.46 = (f32[8,8,8,1]{3,0,2,1:T(8,128)S(1)}, f32[8,8,8,1]{3,0,2,1:T(8,128)S(1)}, u32[]{:S(2)}, u32[]{:S(2)}) collective-permute-start(f32[8,8,8,1]{3,0,2,1:T(8,128)S(1)} %get-tuple-element.298), channel_id=1, source_target_pairs={{1,0},{2,1},{3,2},{5,4},{6,5},{7,6},{9,8},{10,9},{11,10},{13,12},{... | collective-permute-start | bytes 6152 | tf_op jit(solution)/shard_map/ppermute | solution.py:23
  331.3 10.8 %collective-permute-start.51 = (f32[8,8,8,1]{3,0,2,1:T(8,128)S(1)}, f32[8,8,8,1]{3,0,2,1:T(8,128)S(1)}, u32[]{:S(2)}, u32[]{:S(2)}) collective-permute-start(f32[8,8,8,1]{3,0,2,1:T(8,128)S(1)} %get-tuple-element.291), channel_id=1, source_target_pairs={{0,1},{1,2},{2,3},{4,5},{5,6},{6,7},{8,9},{9,10},{10,11},{12,13},{... | collective-permute-start | bytes 6152 | tf_op jit(solution)/shard_map/ppermute | solution.py:21
  333.2 8.9 %collective-permute-start.50 = (f32[8,8,8,1]{3,0,2,1:T(8,128)S(1)}, f32[8,8,8,1]{3,0,2,1:T(8,128)S(1)}, u32[]{:S(2)}, u32[]{:S(2)}) collective-permute-start(f32[8,8,8,1]{3,0,2,1:T(8,128)S(1)} %get-tuple-element.290), channel_id=1, source_target_pairs={{1,0},{2,1},{3,2},{5,4},{6,5},{7,6},{9,8},{10,9},{11,10},{13,12},{... | collective-permute-start | bytes 6152 | tf_op jit(solution)/shard_map/ppermute | solution.py:23
  395.0 12.2 %collective-permute-start.55 = (f32[8,8,8,1]{3,0,2,1:T(8,128)}, f32[8,8,8,1]{3,0,2,1:T(8,128)S(1)}, u32[]{:S(2)}, u32[]{:S(2)}) collective-permute-start(f32[8,8,8,1]{3,0,2,1:T(8,128)} %get-tuple-element.283), channel_id=1, source_target_pairs={{0,1},{1,2},{2,3},{4,5},{5,6},{6,7},{8,9},{9,10},{10,11},{12,13},{... | collective-permute-start | bytes 6152 | tf_op jit(solution)/shard_map/ppermute | solution.py:21
  396.9 10.3 %collective-permute-start.54 = (f32[8,8,8,1]{3,0,2,1:T(8,128)}, f32[8,8,8,1]{3,0,2,1:T(8,128)S(1)}, u32[]{:S(2)}, u32[]{:S(2)}) collective-permute-start(f32[8,8,8,1]{3,0,2,1:T(8,128)} %get-tuple-element.282), channel_id=1, source_target_pairs={{1,0},{2,1},{3,2},{5,4},{6,5},{7,6},{9,8},{10,9},{11,10},{13,12},{... | collective-permute-start | bytes 6152 | tf_op jit(solution)/shard_map/ppermute | solution.py:23
  400.6 6.6 %collective-permute-start.53 = (f32[8,1,8,128]{3,0,2,1:T(8,128)S(1)}, f32[8,1,8,128]{3,0,2,1:T(8,128)S(1)}, u32[]{:S(2)}, u32[]{:S(2)}) collective-permute-start(f32[8,1,8,128]{3,0,2,1:T(8,128)S(1)} %get-tuple-element.277), channel_id=1, source_target_pairs={{0,4},{4,8},{8,12},{12,16},{16,20},{20,24},{24,28},{1,5},{5,9},{9,... | collective-permute-start | bytes 98312 | tf_op jit(solution)/shard_map/ppermute | solution.py:21
  410.0 11.8 %collective-permute-start.59 = (f32[8,8,8,1]{3,0,2,1:T(8,128)S(1)}, f32[8,8,8,1]{3,0,2,1:T(8,128)S(1)}, u32[]{:S(2)}, u32[]{:S(2)}) collective-permute-start(f32[8,8,8,1]{3,0,2,1:T(8,128)S(1)} %get-tuple-element.275), channel_id=1, source_target_pairs={{0,1},{1,2},{2,3},{4,5},{5,6},{6,7},{8,9},{9,10},{10,11},{12,13},{... | collective-permute-start | bytes 6152 | tf_op jit(solution)/shard_map/ppermute | solution.py:21
  411.9 9.8 %collective-permute-start.58 = (f32[8,8,8,1]{3,0,2,1:T(8,128)S(1)}, f32[8,8,8,1]{3,0,2,1:T(8,128)S(1)}, u32[]{:S(2)}, u32[]{:S(2)}) collective-permute-start(f32[8,8,8,1]{3,0,2,1:T(8,128)S(1)} %get-tuple-element.274), channel_id=1, source_target_pairs={{1,0},{2,1},{3,2},{5,4},{6,5},{7,6},{9,8},{10,9},{11,10},{13,12},{... | collective-permute-start | bytes 6152 | tf_op jit(solution)/shard_map/ppermute | solution.py:23
  415.6 6.4 %collective-permute-start.57 = (f32[8,1,8,128]{3,0,2,1:T(8,128)S(1)}, f32[8,1,8,128]{3,0,2,1:T(8,128)S(1)}, u32[]{:S(2)}, u32[]{:S(2)}) collective-permute-start(f32[8,1,8,128]{3,0,2,1:T(8,128)S(1)} %get-tuple-element.269), channel_id=1, source_target_pairs={{0,4},{4,8},{8,12},{12,16},{16,20},{20,24},{24,28},{1,5},{5,9},{9,... | collective-permute-start | bytes 98312 | tf_op jit(solution)/shard_map/ppermute | solution.py:21
  426.8 10.3 %collective-permute-start.63 = (f32[8,8,8,1]{3,0,2,1:T(8,128)S(1)}, f32[8,8,8,1]{3,0,2,1:T(8,128)S(1)}, u32[]{:S(2)}, u32[]{:S(2)}) collective-permute-start(f32[8,8,8,1]{3,0,2,1:T(8,128)S(1)} %get-tuple-element.267), channel_id=1, source_target_pairs={{0,1},{1,2},{2,3},{4,5},{5,6},{6,7},{8,9},{9,10},{10,11},{12,13},{... | collective-permute-start | bytes 6152 | tf_op jit(solution)/shard_map/ppermute | solution.py:21
  428.8 8.3 %collective-permute-start.62 = (f32[8,8,8,1]{3,0,2,1:T(8,128)S(1)}, f32[8,8,8,1]{3,0,2,1:T(8,128)S(1)}, u32[]{:S(2)}, u32[]{:S(2)}) collective-permute-start(f32[8,8,8,1]{3,0,2,1:T(8,128)S(1)} %get-tuple-element.266), channel_id=1, source_target_pairs={{1,0},{2,1},{3,2},{5,4},{6,5},{7,6},{9,8},{10,9},{11,10},{13,12},{... | collective-permute-start | bytes 6152 | tf_op jit(solution)/shard_map/ppermute | solution.py:23
  442.2 10.4 %collective-permute-start.67 = (f32[8,8,8,1]{3,0,2,1:T(8,128)S(1)}, f32[8,8,8,1]{3,0,2,1:T(8,128)S(1)}, u32[]{:S(2)}, u32[]{:S(2)}) collective-permute-start(f32[8,8,8,1]{3,0,2,1:T(8,128)S(1)} %get-tuple-element.259), channel_id=1, source_target_pairs={{0,1},{1,2},{2,3},{4,5},{5,6},{6,7},{8,9},{9,10},{10,11},{12,13},{... | collective-permute-start | bytes 6152 | tf_op jit(solution)/shard_map/ppermute | solution.py:21
  444.2 8.5 %collective-permute-start.66 = (f32[8,8,8,1]{3,0,2,1:T(8,128)S(1)}, f32[8,8,8,1]{3,0,2,1:T(8,128)S(1)}, u32[]{:S(2)}, u32[]{:S(2)}) collective-permute-start(f32[8,8,8,1]{3,0,2,1:T(8,128)S(1)} %get-tuple-element.258), channel_id=1, source_target_pairs={{1,0},{2,1},{3,2},{5,4},{6,5},{7,6},{9,8},{10,9},{11,10},{13,12},{... | collective-permute-start | bytes 6152 | tf_op jit(solution)/shard_map/ppermute | solution.py:23
  515.6 9.5 %collective-permute-start.71 = (f32[8,8,8,1]{3,0,2,1:T(8,128)S(1)}, f32[8,8,8,1]{3,0,2,1:T(8,128)S(1)}, u32[]{:S(2)}, u32[]{:S(2)}) collective-permute-start(f32[8,8,8,1]{3,0,2,1:T(8,128)S(1)} %get-tuple-element.251), channel_id=1, source_target_pairs={{0,1},{1,2},{2,3},{4,5},{5,6},{6,7},{8,9},{9,10},{10,11},{12,13},{... | collective-permute-start | bytes 6152 | tf_op jit(solution)/shard_map/ppermute | solution.py:21
  517.5 7.6 %collective-permute-start.70 = (f32[8,8,8,1]{3,0,2,1:T(8,128)S(1)}, f32[8,8,8,1]{3,0,2,1:T(8,128)S(1)}, u32[]{:S(2)}, u32[]{:S(2)}) collective-permute-start(f32[8,8,8,1]{3,0,2,1:T(8,128)S(1)} %get-tuple-element.250), channel_id=1, source_target_pairs={{1,0},{2,1},{3,2},{5,4},{6,5},{7,6},{9,8},{10,9},{11,10},{13,12},{... | collective-permute-start | bytes 6152 | tf_op jit(solution)/shard_map/ppermute | solution.py:23
  530.7 11.8 %collective-permute-start.75 = (f32[8,8,8,1]{3,0,2,1:T(8,128)S(1)}, f32[8,8,8,1]{3,0,2,1:T(8,128)S(1)}, u32[]{:S(2)}, u32[]{:S(2)}) collective-permute-start(f32[8,8,8,1]{3,0,2,1:T(8,128)S(1)} %get-tuple-element.243), channel_id=1, source_target_pairs={{0,1},{1,2},{2,3},{4,5},{5,6},{6,7},{8,9},{9,10},{10,11},{12,13},{... | collective-permute-start | bytes 6152 | tf_op jit(solution)/shard_map/ppermute | solution.py:21
  532.6 9.8 %collective-permute-start.74 = (f32[8,8,8,1]{3,0,2,1:T(8,128)S(1)}, f32[8,8,8,1]{3,0,2,1:T(8,128)S(1)}, u32[]{:S(2)}, u32[]{:S(2)}) collective-permute-start(f32[8,8,8,1]{3,0,2,1:T(8,128)S(1)} %get-tuple-element.242), channel_id=1, source_target_pairs={{1,0},{2,1},{3,2},{5,4},{6,5},{7,6},{9,8},{10,9},{11,10},{13,12},{... | collective-permute-start | bytes 6152 | tf_op jit(solution)/shard_map/ppermute | solution.py:23
  547.5 9.8 %collective-permute-start.79 = (f32[8,8,8,1]{3,0,2,1:T(8,128)S(1)}, f32[8,8,8,1]{3,0,2,1:T(8,128)S(1)}, u32[]{:S(2)}, u32[]{:S(2)}) collective-permute-start(f32[8,8,8,1]{3,0,2,1:T(8,128)S(1)} %get-tuple-element.235), channel_id=1, source_target_pairs={{0,1},{1,2},{2,3},{4,5},{5,6},{6,7},{8,9},{9,10},{10,11},{12,13},{... | collective-permute-start | bytes 6152 | tf_op jit(solution)/shard_map/ppermute | solution.py:21
  549.5 7.8 %collective-permute-start.78 = (f32[8,8,8,1]{3,0,2,1:T(8,128)S(1)}, f32[8,8,8,1]{3,0,2,1:T(8,128)S(1)}, u32[]{:S(2)}, u32[]{:S(2)}) collective-permute-start(f32[8,8,8,1]{3,0,2,1:T(8,128)S(1)} %get-tuple-element.234), channel_id=1, source_target_pairs={{1,0},{2,1},{3,2},{5,4},{6,5},{7,6},{9,8},{10,9},{11,10},{13,12},{... | collective-permute-start | bytes 6152 | tf_op jit(solution)/shard_map/ppermute | solution.py:23
  562.4 11.7 %collective-permute-start.83 = (f32[8,8,8,1]{3,0,2,1:T(8,128)S(1)}, f32[8,8,8,1]{3,0,2,1:T(8,128)S(1)}, u32[]{:S(2)}, u32[]{:S(2)}) collective-permute-start(f32[8,8,8,1]{3,0,2,1:T(8,128)S(1)} %get-tuple-element.227), channel_id=1, source_target_pairs={{0,1},{1,2},{2,3},{4,5},{5,6},{6,7},{8,9},{9,10},{10,11},{12,13},{... | collective-permute-start | bytes 6152 | tf_op jit(solution)/shard_map/ppermute | solution.py:21
  564.3 9.8 %collective-permute-start.82 = (f32[8,8,8,1]{3,0,2,1:T(8,128)S(1)}, f32[8,8,8,1]{3,0,2,1:T(8,128)S(1)}, u32[]{:S(2)}, u32[]{:S(2)}) collective-permute-start(f32[8,8,8,1]{3,0,2,1:T(8,128)S(1)} %get-tuple-element.226), channel_id=1, source_target_pairs={{1,0},{2,1},{3,2},{5,4},{6,5},{7,6},{9,8},{10,9},{11,10},{13,12},{... | collective-permute-start | bytes 6152 | tf_op jit(solution)/shard_map/ppermute | solution.py:23
  (41 other events, 232.5 us)
where the time goes:
time: 591 us; the launch traced here: 579 us
  starting transfers between devices  221 us (37%)
  blocking collectives  201 us (34%)
  waiting for transfers between devices  83.3 us (14%)
  other arithmetic  33.3 us (6%)
  local copies, waits for them, and re-layouts  18.9 us (3%)
  matrix products  17.9 us (3%)
    psum x4, blocking collectives, body(): lax.psum((jnp.stack([product(work, basis[i]) for i in range(step + 1)]),...  159 us
    ppermute x42, starting transfers between devices, with_halo(): lax.ppermute(tail, axis, [(i, (i + 1) % count) for i in range(ends)])  117 us
    ppermute x42, starting transfers between devices, with_halo(): lax.ppermute(head, axis, [((i + 1) % count, i) for i in range(ends)])  104 us
    ppermute x42, waiting for transfers between devices, with_halo(): lax.ppermute(head, axis, [((i + 1) % count, i) for i in range(ends)])  80.1 us
    psum x1, blocking collectives, body(): lead = jnp.linalg.cholesky(lax.psum(product(start, start), ('sub', 'slab')))  42.4 us
  transfers between devices with their start and end apart: 84, of which 35 were waited for; matrix products, arithmetic and copies ran while one was open for 3% of the time, Pallas kernels for 0%

commit v1 on v0

--- a/solution.py
+++ b/solution.py
@@ -128,8 +128,14 @@
         direction = precondition(basis[step], operate, inv_diag)
         work = operate(direction)
         stacked, whole = lax.psum(
-            (jnp.stack([product(work, basis[i]) for i in range(step + 1)]), product(work, work)),
-            ("sub", "slab"),
+            lax.psum(
+                (
+                    jnp.stack([product(work, basis[i]) for i in range(step + 1)]),
+                    product(work, work),
+                ),
+                "slab",
+            ),
+            "sub",
         )
         found = [stacked[i] for i in range(step + 1)]
         block = whole

time: 591 us -> 573 us (0.970)
  starting transfers between devices: 221 us -> 206 us
    psum x4, blocking collectives: 159 us -> 36.4 us  [body(): lax.psum((jnp.stack([product(work, basis[i]) for i in range(step + 1)]),...]
    psum x0 -> x4, blocking collectives: none -> 120 us  [body(): lax.psum(lax.psum((jnp.stack([product(work, basis[i]) for i in range(step...]
    ppermute x42, starting transfers between devices: 117 us -> 102 us  [with_halo(): lax.ppermute(tail, axis, [(i, (i + 1) % count) for i in range(ends)])]
where the time goes in v1:
time: 573 us; the launch traced here: 562 us
  starting transfers between devices  206 us (36%)
  blocking collectives  199 us (35%)
  waiting for transfers between devices  82.3 us (14%)
  other arithmetic  33.3 us (6%)
  local copies, waits for them, and re-layouts  18.8 us (3%)
  matrix products  17.9 us (3%)
    psum x4, blocking collectives, body(): lax.psum(lax.psum((jnp.stack([product(work, basis[i]) for i in range(step...  120 us
    ppermute x42, starting transfers between devices, with_halo(): lax.ppermute(head, axis, [((i + 1) % count, i) for i in range(ends)])  104 us
    ppermute x42, starting transfers between devices, with_halo(): lax.ppermute(tail, axis, [(i, (i + 1) % count) for i in range(ends)])  102 us
    ppermute x42, waiting for transfers between devices, with_halo(): lax.ppermute(head, axis, [((i + 1) % count, i) for i in range(ends)])  79.3 us
    psum x1, blocking collectives, body(): lead = jnp.linalg.cholesky(lax.psum(product(start, start), ('sub', 'slab')))  42.4 us
    psum x4, blocking collectives, body(): lax.psum((jnp.stack([product(work, basis[i]) for i in range(step + 1)]),...  36.4 us
  transfers between devices with their start and end apart: 84, of which 35 were waited for; matrix products, arithmetic and copies ran while one was open for 3% of the time, Pallas kernels for 0%

profile of v1, /device:TPU:2, one launch (start us, length us, event | category | flops | bytes accessed | tf_op | source)
XLA Modules:
  0.0 562.2 jit_solution(10255116856603378751)
XLA Ops:
  3.5 3.6 collective-permute-start.2
  16.0 42.4 %psum.119 = f32[8,8]{0,1:T(8,128)S(1)} all-reduce(f32[8,8]{0,1:T(8,128)S(1)} %convolution_bitcast_fusion.14), channel_id=1, replica_groups=mesh['sub'=8,'slab'=4] {'sub','slab'}, use_global_device_ids=true, to_apply=%region_0.1 | all-reduce | flops 64 | bytes 512 | tf_op jit(solution)/shard_map/psum | solution.py:123
  66.3 3.6 collective-permute-start.6
  74.8 4.2 collective-permute-done.4
  81.6 3.6 collective-permute-start.10
  85.2 4.4 collective-permute-start.9
  91.2 4.2 collective-permute-done.8
  98.0 3.6 collective-permute-start.14
  106.6 4.2 collective-permute-done.12
  113.4 3.6 collective-permute-start.18
  117.1 4.2 collective-permute-start.17
  122.9 4.2 collective-permute-done.16
  128.8 5.9 %all-reduce.93 = (f32[1,8,8]{2,1,0:T(8,128)S(1)}, f32[8,8]{0,1:T(8,128)S(1)}) all-reduce(f32[1,8,8]{2,1,0:T(8,128)S(1)} %convolution_bitcast_fusion.13, f32[8,8]{0,1:T(8,128)S(1)} %convolution_bitcast_fusion.12), channel_id=1, replica_groups=mesh['sub'=8,'slab'=4] {'slab'}, use_global_device_ids=true, to_apply=%region_3.6 | all-reduce | flops 128 | bytes 1024 | tf_op jit(solution)/shard_map/psum | solution.py:131
  134.7 18.9 %all-reduce.89 = (f32[8,8]{1,0:T(8,128)S(1)}, f32[8,8]{0,1:T(8,128)S(1)}) all-reduce(f32[8,8]{1,0:T(8,128)S(1)} %bitcast.463, f32[8,8]{0,1:T(8,128)S(1)} %get-tuple-element.201), channel_id=1, replica_groups=mesh['sub'=8,'slab'=4] {'sub'}, use_global_device_ids=true, to_apply=%region_4.7 | all-reduce | flops 128 | bytes 1024 | tf_op jit(solution)/shard_map/psum | solution.py:130
  162.1 3.6 collective-permute-start.22
  176.5 3.6 collective-permute-start.26
  184.6 4.2 collective-permute-done.24
  191.4 3.6 collective-permute-start.30
  199.5 4.2 collective-permute-done.28
  206.3 3.6 collective-permute-start.34
  214.4 4.2 collective-permute-done.32
  221.1 10.1 %all-reduce.92 = (f32[2,8,8]{2,1,0:T(8,128)S(1)}, f32[8,8]{0,1:T(8,128)S(1)}) all-reduce(f32[2,8,8]{2,1,0:T(8,128)S(1)} %pad_maximum_fusion.44, f32[8,8]{0,1:T(8,128)S(1)} %convolution_bitcast_fusion.9), channel_id=1, replica_groups=mesh['sub'=8,'slab'=4] {'slab'}, use_global_device_ids=true, to_apply=%region_8.11 | all-reduce | flops 192 | bytes 1536 | tf_op jit(solution)/shard_map/psum | solution.py:131
  231.2 33.8 %all-reduce.88 = (f32[2,8,8]{2,1,0:T(8,128)S(1)}, f32[8,8]{0,1:T(8,128)S(1)}) all-reduce(f32[2,8,8]{2,1,0:T(8,128)S(1)} %get-tuple-element.198, f32[8,8]{0,1:T(8,128)S(1)} %get-tuple-element.199), channel_id=1, replica_groups=mesh['sub'=8,'slab'=4] {'sub'}, use_global_device_ids=true, to_apply=%region_9.12 | all-reduce | flops 192 | bytes 1536 | tf_op jit(solution)/shard_map/psum | solution.py:130
  272.2 3.6 collective-permute-start.38
  285.4 3.6 collective-permute-start.42
  294.3 4.2 collective-permute-done.40
  301.1 3.6 collective-permute-start.46
  309.1 4.2 collective-permute-done.44
  316.0 3.6 collective-permute-start.50
  324.0 4.2 collective-permute-done.48
  331.5 10.1 %all-reduce.91 = (f32[3,8,8]{2,1,0:T(8,128)S(1)}, f32[8,8]{0,1:T(8,128)S(1)}) all-reduce(f32[3,8,8]{2,1,0:T(8,128)S(1)} %pad_maximum_fusion.43, f32[8,8]{0,1:T(8,128)S(1)} %convolution_bitcast_fusion.5), channel_id=1, replica_groups=mesh['sub'=8,'slab'=4] {'slab'}, use_global_device_ids=true, to_apply=%region_12.15 | all-reduce | flops 256 | bytes 2048 | tf_op jit(solution)/shard_map/psum | solution.py:131
  341.6 33.9 %all-reduce.87 = (f32[3,8,8]{2,1,0:T(8,128)S(1)}, f32[8,8]{0,1:T(8,128)S(1)}) all-reduce(f32[3,8,8]{2,1,0:T(8,128)S(1)} %get-tuple-element.196, f32[8,8]{0,1:T(8,128)S(1)} %get-tuple-element.197), channel_id=1, replica_groups=mesh['sub'=8,'slab'=4] {'sub'}, use_global_device_ids=true, to_apply=%region_13.16 | all-reduce | flops 256 | bytes 2048 | tf_op jit(solution)/shard_map/psum | solution.py:130
  396.5 3.6 collective-permute-start.58
  400.1 3.6 collective-permute-start.57
  405.4 4.2 collective-permute-done.56
  412.2 3.6 collective-permute-start.62
  420.7 4.2 collective-permute-done.60
  427.6 3.6 collective-permute-start.66
  435.6 4.2 collective-permute-done.64
  443.8 10.3 %all-reduce.90 = (f32[4,8,8]{2,1,0:T(8,128)S(1)}, f32[8,8]{0,1:T(8,128)S(1)}) all-reduce(f32[4,8,8]{2,1,0:T(8,128)S(1)} %pad_maximum_fusion.42, f32[8,8]{0,1:T(8,128)S(1)} %convolution_bitcast_fusion), channel_id=1, replica_groups=mesh['sub'=8,'slab'=4] {'slab'}, use_global_device_ids=true, to_apply=%region_16.19 | all-reduce | flops 320 | bytes 2560 | tf_op jit(solution)/shard_map/psum | solution.py:131
  454.0 33.8 %all-reduce.86 = (f32[4,8,8]{2,1,0:T(8,128)S(1)}, f32[8,8]{0,1:T(8,128)S(1)}) all-reduce(f32[4,8,8]{2,1,0:T(8,128)S(1)} %get-tuple-element.194, f32[8,8]{0,1:T(8,128)S(1)} %get-tuple-element.195), channel_id=1, replica_groups=mesh['sub'=8,'slab'=4] {'sub'}, use_global_device_ids=true, to_apply=%region_17.20 | all-reduce | flops 320 | bytes 2560 | tf_op jit(solution)/shard_map/psum | solution.py:130
  504.4 3.6 collective-permute-start.70
  517.8 3.6 collective-permute-start.74
  526.6 4.2 collective-permute-done.72
  533.4 3.6 collective-permute-start.78
  541.5 4.2 collective-permute-done.76
  548.3 3.6 collective-permute-start.82
  556.9 3.7 collective-permute-done.80
  (367 shorter events, 206.3 us)
Async XLA Ops:
  1.6 61.9 %collective-permute-start.3 = (f32[1,8,8,1]{3,2,1,0:T(8,128)S(1)}, f32[1,8,8,1]{3,2,1,0:T(8,128)S(1)}, u32[]{:S(2)}, u32[]{:S(2)}) collective-permute-start(f32[1,8,8,1]{3,2,1,0:T(8,128)S(1)} %get-tuple-element.401), channel_id=1, source_target_pairs={{0,1},{1,2},{2,3},{4,5},{5,6},{6,7},{8,9},{9,10},{10,11},{12,13},{... | collective-permute-start | bytes 776 | tf_op jit(solution)/shard_map/ppermute | solution.py:21
  3.5 60.0 %collective-permute-start.2 = (f32[1,8,8,1]{3,2,1,0:T(8,128)S(1)}, f32[1,8,8,1]{3,2,1,0:T(8,128)S(1)}, u32[]{:S(2)}, u32[]{:S(2)}) collective-permute-start(f32[1,8,8,1]{3,2,1,0:T(8,128)S(1)} %get-tuple-element.400), channel_id=1, source_target_pairs={{1,0},{2,1},{3,2},{5,4},{6,5},{7,6},{9,8},{10,9},{11,10},{13,12},{... | collective-permute-start | bytes 776 | tf_op jit(solution)/shard_map/ppermute | solution.py:23
  9.1 54.5 %collective-permute-start.1 = (f32[1,1,8,128]{3,2,1,0:T(8,128)S(1)}, f32[1,1,8,128]{3,2,1,0:T(8,128)S(1)}, u32[]{:S(2)}, u32[]{:S(2)}) collective-permute-start(f32[1,1,8,128]{3,2,1,0:T(8,128)S(1)} %fusion.154), channel_id=1, source_target_pairs={{0,4},{4,8},{8,12},{12,16},{16,20},{20,24},{24,28},{1,5},{5,9},{9,... | collective-permute-start | bytes 12296 | tf_op jit(solution)/shard_map/ppermute | solution.py:21
  12.6 51.0 %collective-permute-start = (f32[1,1,8,128]{3,2,1,0:T(8,128)S(1)}, f32[1,1,8,128]{3,2,1,0:T(8,128)S(1)}, u32[]{:S(2)}, u32[]{:S(2)}) collective-permute-start(f32[1,1,8,128]{3,2,1,0:T(8,128)S(1)} %slice.1210), channel_id=1, source_target_pairs={{4,0},{8,4},{12,8},{16,12},{20,16},{24,20},{28,24},{5,1},{9,5},{13... | collective-permute-start | bytes 12296 | tf_op jit(solution)/shard_map/ppermute | solution.py:23
  64.4 10.3 %collective-permute-start.7 = (f32[8,8,8,1]{3,0,2,1:T(8,128)S(1)}, f32[8,8,8,1]{3,0,2,1:T(8,128)S(1)}, u32[]{:S(2)}, u32[]{:S(2)}) collective-permute-start(f32[8,8,8,1]{3,0,2,1:T(8,128)S(1)} %get-tuple-element.387), channel_id=1, source_target_pairs={{0,1},{1,2},{2,3},{4,5},{5,6},{6,7},{8,9},{9,10},{10,11},{12,13},{... | collective-permute-start | bytes 6152 | tf_op jit(solution)/shard_map/ppermute | solution.py:21
  66.3 8.4 %collective-permute-start.6 = (f32[8,8,8,1]{3,0,2,1:T(8,128)S(1)}, f32[8,8,8,1]{3,0,2,1:T(8,128)S(1)}, u32[]{:S(2)}, u32[]{:S(2)}) collective-permute-start(f32[8,8,8,1]{3,0,2,1:T(8,128)S(1)} %get-tuple-element.386), channel_id=1, source_target_pairs={{1,0},{2,1},{3,2},{5,4},{6,5},{7,6},{9,8},{10,9},{11,10},{13,12},{... | collective-permute-start | bytes 6152 | tf_op jit(solution)/shard_map/ppermute | solution.py:23
  73.2 5.8 %collective-permute-start.4 = (f32[8,1,8,128]{3,0,2,1:T(8,128)S(1)}, f32[8,1,8,128]{3,0,2,1:T(8,128)S(1)}, u32[]{:S(2)}, u32[]{:S(2)}) collective-permute-start(f32[8,1,8,128]{3,0,2,1:T(8,128)S(1)} %get-tuple-element.380), channel_id=1, source_target_pairs={{4,0},{8,4},{12,8},{16,12},{20,16},{24,20},{28,24},{5,1},{9,5},{13... | collective-permute-start | bytes 98312 | tf_op jit(solution)/shard_map/ppermute | solution.py:23
  79.6 11.4 %collective-permute-start.11 = (f32[8,8,8,1]{3,0,2,1:T(8,128)S(1)}, f32[8,8,8,1]{3,0,2,1:T(8,128)S(1)}, u32[]{:S(2)}, u32[]{:S(2)}) collective-permute-start(f32[8,8,8,1]{3,0,2,1:T(8,128)S(1)} %get-tuple-element.379), channel_id=1, source_target_pairs={{0,1},{1,2},{2,3},{4,5},{5,6},{6,7},{8,9},{9,10},{10,11},{12,13},{... | collective-permute-start | bytes 6152 | tf_op jit(solution)/shard_map/ppermute | solution.py:21
  81.6 9.4 %collective-permute-start.10 = (f32[8,8,8,1]{3,0,2,1:T(8,128)S(1)}, f32[8,8,8,1]{3,0,2,1:T(8,128)S(1)}, u32[]{:S(2)}, u32[]{:S(2)}) collective-permute-start(f32[8,8,8,1]{3,0,2,1:T(8,128)S(1)} %get-tuple-element.378), channel_id=1, source_target_pairs={{1,0},{2,1},{3,2},{5,4},{6,5},{7,6},{9,8},{10,9},{11,10},{13,12},{... | collective-permute-start | bytes 6152 | tf_op jit(solution)/shard_map/ppermute | solution.py:23
  85.2 6.0 %collective-permute-start.9 = (f32[8,1,8,128]{3,0,2,1:T(8,128)S(1)}, f32[8,1,8,128]{3,0,2,1:T(8,128)S(1)}, u32[]{:S(2)}, u32[]{:S(2)}) collective-permute-start(f32[8,1,8,128]{3,0,2,1:T(8,128)S(1)} %get-tuple-element.373), channel_id=1, source_target_pairs={{0,4},{4,8},{8,12},{12,16},{16,20},{20,24},{24,28},{1,5},{5,9},{9,... | collective-permute-start | bytes 98312 | tf_op jit(solution)/shard_map/ppermute | solution.py:21
  89.6 5.8 %collective-permute-start.8 = (f32[8,1,8,128]{3,0,2,1:T(8,128)S(1)}, f32[8,1,8,128]{3,0,2,1:T(8,128)S(1)}, u32[]{:S(2)}, u32[]{:S(2)}) collective-permute-start(f32[8,1,8,128]{3,0,2,1:T(8,128)S(1)} %get-tuple-element.372), channel_id=1, source_target_pairs={{4,0},{8,4},{12,8},{16,12},{20,16},{24,20},{28,24},{5,1},{9,5},{13... | collective-permute-start | bytes 98312 | tf_op jit(solution)/shard_map/ppermute | solution.py:23
  96.1 10.3 %collective-permute-start.15 = (f32[8,8,8,1]{3,0,2,1:T(8,128)S(1)}, f32[8,8,8,1]{3,0,2,1:T(8,128)S(1)}, u32[]{:S(2)}, u32[]{:S(2)}) collective-permute-start(f32[8,8,8,1]{3,0,2,1:T(8,128)S(1)} %get-tuple-element.371), channel_id=1, source_target_pairs={{0,1},{1,2},{2,3},{4,5},{5,6},{6,7},{8,9},{9,10},{10,11},{12,13},{... | collective-permute-start | bytes 6152 | tf_op jit(solution)/shard_map/ppermute | solution.py:21
  98.0 8.4 %collective-permute-start.14 = (f32[8,8,8,1]{3,0,2,1:T(8,128)S(1)}, f32[8,8,8,1]{3,0,2,1:T(8,128)S(1)}, u32[]{:S(2)}, u32[]{:S(2)}) collective-permute-start(f32[8,8,8,1]{3,0,2,1:T(8,128)S(1)} %get-tuple-element.370), channel_id=1, source_target_pairs={{1,0},{2,1},{3,2},{5,4},{6,5},{7,6},{9,8},{10,9},{11,10},{13,12},{... | collective-permute-start | bytes 6152 | tf_op jit(solution)/shard_map/ppermute | solution.py:23
  105.1 5.8 %collective-permute-start.12 = (f32[8,1,8,128]{3,0,2,1:T(8,128)S(1)}, f32[8,1,8,128]{3,0,2,1:T(8,128)S(1)}, u32[]{:S(2)}, u32[]{:S(2)}) collective-permute-start(f32[8,1,8,128]{3,0,2,1:T(8,128)S(1)} %get-tuple-element.364), channel_id=1, source_target_pairs={{4,0},{8,4},{12,8},{16,12},{20,16},{24,20},{28,24},{5,1},{9,5},{13... | collective-permute-start | bytes 98312 | tf_op jit(solution)/shard_map/ppermute | solution.py:23
  111.5 11.1 %collective-permute-start.19 = (f32[8,8,8,1]{3,0,2,1:T(8,128)S(1)}, f32[8,8,8,1]{3,0,2,1:T(8,128)S(1)}, u32[]{:S(2)}, u32[]{:S(2)}) collective-permute-start(f32[8,8,8,1]{3,0,2,1:T(8,128)S(1)} %get-tuple-element.363), channel_id=1, source_target_pairs={{0,1},{1,2},{2,3},{4,5},{5,6},{6,7},{8,9},{9,10},{10,11},{12,13},{... | collective-permute-start | bytes 6152 | tf_op jit(solution)/shard_map/ppermute | solution.py:21
  113.4 9.2 %collective-permute-start.18 = (f32[8,8,8,1]{3,0,2,1:T(8,128)S(1)}, f32[8,8,8,1]{3,0,2,1:T(8,128)S(1)}, u32[]{:S(2)}, u32[]{:S(2)}) collective-permute-start(f32[8,8,8,1]{3,0,2,1:T(8,128)S(1)} %get-tuple-element.362), channel_id=1, source_target_pairs={{1,0},{2,1},{3,2},{5,4},{6,5},{7,6},{9,8},{10,9},{11,10},{13,12},{... | collective-permute-start | bytes 6152 | tf_op jit(solution)/shard_map/ppermute | solution.py:23
  160.2 11.2 %collective-permute-start.23 = (f32[8,8,8,1]{3,0,2,1:T(8,128)}, f32[8,8,8,1]{3,0,2,1:T(8,128)S(1)}, u32[]{:S(2)}, u32[]{:S(2)}) collective-permute-start(f32[8,8,8,1]{3,0,2,1:T(8,128)} %get-tuple-element.355), channel_id=1, source_target_pairs={{0,1},{1,2},{2,3},{4,5},{5,6},{6,7},{8,9},{9,10},{10,11},{12,13},{... | collective-permute-start | bytes 6152 | tf_op jit(solution)/shard_map/ppermute | solution.py:21
  162.1 9.3 %collective-permute-start.22 = (f32[8,8,8,1]{3,0,2,1:T(8,128)S(1)}, f32[8,8,8,1]{3,0,2,1:T(8,128)S(1)}, u32[]{:S(2)}, u32[]{:S(2)}) collective-permute-start(f32[8,8,8,1]{3,0,2,1:T(8,128)S(1)} %get-tuple-element.354), channel_id=1, source_target_pairs={{1,0},{2,1},{3,2},{5,4},{6,5},{7,6},{9,8},{10,9},{11,10},{13,12},{... | collective-permute-start | bytes 6152 | tf_op jit(solution)/shard_map/ppermute | solution.py:23
  174.6 9.8 %collective-permute-start.27 = (f32[8,8,8,1]{3,0,2,1:T(8,128)S(1)}, f32[8,8,8,1]{3,0,2,1:T(8,128)S(1)}, u32[]{:S(2)}, u32[]{:S(2)}) collective-permute-start(f32[8,8,8,1]{3,0,2,1:T(8,128)S(1)} %get-tuple-element.347), channel_id=1, source_target_pairs={{0,1},{1,2},{2,3},{4,5},{5,6},{6,7},{8,9},{9,10},{10,11},{12,13},{... | collective-permute-start | bytes 6152 | tf_op jit(solution)/shard_map/ppermute | solution.py:21
  176.5 7.8 %collective-permute-start.26 = (f32[8,8,8,1]{3,0,2,1:T(8,128)S(1)}, f32[8,8,8,1]{3,0,2,1:T(8,128)S(1)}, u32[]{:S(2)}, u32[]{:S(2)}) collective-permute-start(f32[8,8,8,1]{3,0,2,1:T(8,128)S(1)} %get-tuple-element.346), channel_id=1, source_target_pairs={{1,0},{2,1},{3,2},{5,4},{6,5},{7,6},{9,8},{10,9},{11,10},{13,12},{... | collective-permute-start | bytes 6152 | tf_op jit(solution)/shard_map/ppermute | solution.py:23
  189.4 9.8 %collective-permute-start.31 = (f32[8,8,8,1]{3,0,2,1:T(8,128)S(1)}, f32[8,8,8,1]{3,0,2,1:T(8,128)S(1)}, u32[]{:S(2)}, u32[]{:S(2)}) collective-permute-start(f32[8,8,8,1]{3,0,2,1:T(8,128)S(1)} %get-tuple-element.339), channel_id=1, source_target_pairs={{0,1},{1,2},{2,3},{4,5},{5,6},{6,7},{8,9},{9,10},{10,11},{12,13},{... | collective-permute-start | bytes 6152 | tf_op jit(solution)/shard_map/ppermute | solution.py:21
  191.4 7.9 %collective-permute-start.30 = (f32[8,8,8,1]{3,0,2,1:T(8,128)S(1)}, f32[8,8,8,1]{3,0,2,1:T(8,128)S(1)}, u32[]{:S(2)}, u32[]{:S(2)}) collective-permute-start(f32[8,8,8,1]{3,0,2,1:T(8,128)S(1)} %get-tuple-element.338), channel_id=1, source_target_pairs={{1,0},{2,1},{3,2},{5,4},{6,5},{7,6},{9,8},{10,9},{11,10},{13,12},{... | collective-permute-start | bytes 6152 | tf_op jit(solution)/shard_map/ppermute | solution.py:23
  204.4 9.9 %collective-permute-start.35 = (f32[8,8,8,1]{3,0,2,1:T(8,128)S(1)}, f32[8,8,8,1]{3,0,2,1:T(8,128)S(1)}, u32[]{:S(2)}, u32[]{:S(2)}) collective-permute-start(f32[8,8,8,1]{3,0,2,1:T(8,128)S(1)} %get-tuple-element.331), channel_id=1, source_target_pairs={{0,1},{1,2},{2,3},{4,5},{5,6},{6,7},{8,9},{9,10},{10,11},{12,13},{... | collective-permute-start | bytes 6152 | tf_op jit(solution)/shard_map/ppermute | solution.py:21
  206.3 8.0 %collective-permute-start.34 = (f32[8,8,8,1]{3,0,2,1:T(8,128)S(1)}, f32[8,8,8,1]{3,0,2,1:T(8,128)S(1)}, u32[]{:S(2)}, u32[]{:S(2)}) collective-permute-start(f32[8,8,8,1]{3,0,2,1:T(8,128)S(1)} %get-tuple-element.330), channel_id=1, source_target_pairs={{1,0},{2,1},{3,2},{5,4},{6,5},{7,6},{9,8},{10,9},{11,10},{13,12},{... | collective-permute-start | bytes 6152 | tf_op jit(solution)/shard_map/ppermute | solution.py:23
  270.2 9.8 %collective-permute-start.39 = (f32[8,8,8,1]{3,0,2,1:T(8,128)}, f32[8,8,8,1]{3,0,2,1:T(8,128)S(1)}, u32[]{:S(2)}, u32[]{:S(2)}) collective-permute-start(f32[8,8,8,1]{3,0,2,1:T(8,128)} %get-tuple-element.323), channel_id=1, source_target_pairs={{0,1},{1,2},{2,3},{4,5},{5,6},{6,7},{8,9},{9,10},{10,11},{12,13},{... | collective-permute-start | bytes 6152 | tf_op jit(solution)/shard_map/ppermute | solution.py:21
  272.2 7.8 %collective-permute-start.38 = (f32[8,8,8,1]{3,0,2,1:T(8,128)S(1)}, f32[8,8,8,1]{3,0,2,1:T(8,128)S(1)}, u32[]{:S(2)}, u32[]{:S(2)}) collective-permute-start(f32[8,8,8,1]{3,0,2,1:T(8,128)S(1)} %get-tuple-element.322), channel_id=1, source_target_pairs={{1,0},{2,1},{3,2},{5,4},{6,5},{7,6},{9,8},{10,9},{11,10},{13,12},{... | collective-permute-start | bytes 6152 | tf_op jit(solution)/shard_map/ppermute | solution.py:23
  283.5 10.6 %collective-permute-start.43 = (f32[8,8,8,1]{3,0,2,1:T(8,128)S(1)}, f32[8,8,8,1]{3,0,2,1:T(8,128)S(1)}, u32[]{:S(2)}, u32[]{:S(2)}) collective-permute-start(f32[8,8,8,1]{3,0,2,1:T(8,128)S(1)} %get-tuple-element.315), channel_id=1, source_target_pairs={{0,1},{1,2},{2,3},{4,5},{5,6},{6,7},{8,9},{9,10},{10,11},{12,13},{... | collective-permute-start | bytes 6152 | tf_op jit(solution)/shard_map/ppermute | solution.py:21
  285.4 8.6 %collective-permute-start.42 = (f32[8,8,8,1]{3,0,2,1:T(8,128)S(1)}, f32[8,8,8,1]{3,0,2,1:T(8,128)S(1)}, u32[]{:S(2)}, u32[]{:S(2)}) collective-permute-start(f32[8,8,8,1]{3,0,2,1:T(8,128)S(1)} %get-tuple-element.314), channel_id=1, source_target_pairs={{1,0},{2,1},{3,2},{5,4},{6,5},{7,6},{9,8},{10,9},{11,10},{13,12},{... | collective-permute-start | bytes 6152 | tf_op jit(solution)/shard_map/ppermute | solution.py:23
  299.2 9.8 %collective-permute-start.47 = (f32[8,8,8,1]{3,0,2,1:T(8,128)S(1)}, f32[8,8,8,1]{3,0,2,1:T(8,128)S(1)}, u32[]{:S(2)}, u32[]{:S(2)}) collective-permute-start(f32[8,8,8,1]{3,0,2,1:T(8,128)S(1)} %get-tuple-element.307), channel_id=1, source_target_pairs={{0,1},{1,2},{2,3},{4,5},{5,6},{6,7},{8,9},{9,10},{10,11},{12,13},{... | collective-permute-start | bytes 6152 | tf_op jit(solution)/shard_map/ppermute | solution.py:21
  301.1 7.8 %collective-permute-start.46 = (f32[8,8,8,1]{3,0,2,1:T(8,128)S(1)}, f32[8,8,8,1]{3,0,2,1:T(8,128)S(1)}, u32[]{:S(2)}, u32[]{:S(2)}) collective-permute-start(f32[8,8,8,1]{3,0,2,1:T(8,128)S(1)} %get-tuple-element.306), channel_id=1, source_target_pairs={{1,0},{2,1},{3,2},{5,4},{6,5},{7,6},{9,8},{10,9},{11,10},{13,12},{... | collective-permute-start | bytes 6152 | tf_op jit(solution)/shard_map/ppermute | solution.py:23
  314.0 9.8 %collective-permute-start.51 = (f32[8,8,8,1]{3,0,2,1:T(8,128)S(1)}, f32[8,8,8,1]{3,0,2,1:T(8,128)S(1)}, u32[]{:S(2)}, u32[]{:S(2)}) collective-permute-start(f32[8,8,8,1]{3,0,2,1:T(8,128)S(1)} %get-tuple-element.299), channel_id=1, source_target_pairs={{0,1},{1,2},{2,3},{4,5},{5,6},{6,7},{8,9},{9,10},{10,11},{12,13},{... | collective-permute-start | bytes 6152 | tf_op jit(solution)/shard_map/ppermute | solution.py:21
  316.0 7.8 %collective-permute-start.50 = (f32[8,8,8,1]{3,0,2,1:T(8,128)S(1)}, f32[8,8,8,1]{3,0,2,1:T(8,128)S(1)}, u32[]{:S(2)}, u32[]{:S(2)}) collective-permute-start(f32[8,8,8,1]{3,0,2,1:T(8,128)S(1)} %get-tuple-element.298), channel_id=1, source_target_pairs={{1,0},{2,1},{3,2},{5,4},{6,5},{7,6},{9,8},{10,9},{11,10},{13,12},{... | collective-permute-start | bytes 6152 | tf_op jit(solution)/shard_map/ppermute | solution.py:23
  381.3 10.5 %collective-permute-start.55 = (f32[8,8,8,1]{3,0,2,1:T(8,128)}, f32[8,8,8,1]{3,0,2,1:T(8,128)S(1)}, u32[]{:S(2)}, u32[]{:S(2)}) collective-permute-start(f32[8,8,8,1]{3,0,2,1:T(8,128)} %get-tuple-element.291), channel_id=1, source_target_pairs={{0,1},{1,2},{2,3},{4,5},{5,6},{6,7},{8,9},{9,10},{10,11},{12,13},{... | collective-permute-start | bytes 6152 | tf_op jit(solution)/shard_map/ppermute | solution.py:21
  383.2 8.6 %collective-permute-start.54 = (f32[8,8,8,1]{3,0,2,1:T(8,128)}, f32[8,8,8,1]{3,0,2,1:T(8,128)S(1)}, u32[]{:S(2)}, u32[]{:S(2)}) collective-permute-start(f32[8,8,8,1]{3,0,2,1:T(8,128)} %get-tuple-element.290), channel_id=1, source_target_pairs={{1,0},{2,1},{3,2},{5,4},{6,5},{7,6},{9,8},{10,9},{11,10},{13,12},{... | collective-permute-start | bytes 6152 | tf_op jit(solution)/shard_map/ppermute | solution.py:23
  394.5 10.6 %collective-permute-start.59 = (f32[8,8,8,1]{3,0,2,1:T(8,128)S(1)}, f32[8,8,8,1]{3,0,2,1:T(8,128)S(1)}, u32[]{:S(2)}, u32[]{:S(2)}) collective-permute-start(f32[8,8,8,1]{3,0,2,1:T(8,128)S(1)} %get-tuple-element.283), channel_id=1, source_target_pairs={{0,1},{1,2},{2,3},{4,5},{5,6},{6,7},{8,9},{9,10},{10,11},{12,13},{... | collective-permute-start | bytes 6152 | tf_op jit(solution)/shard_map/ppermute | solution.py:21
  396.5 8.7 %collective-permute-start.58 = (f32[8,8,8,1]{3,0,2,1:T(8,128)S(1)}, f32[8,8,8,1]{3,0,2,1:T(8,128)S(1)}, u32[]{:S(2)}, u32[]{:S(2)}) collective-permute-start(f32[8,8,8,1]{3,0,2,1:T(8,128)S(1)} %get-tuple-element.282), channel_id=1, source_target_pairs={{1,0},{2,1},{3,2},{5,4},{6,5},{7,6},{9,8},{10,9},{11,10},{13,12},{... | collective-permute-start | bytes 6152 | tf_op jit(solution)/shard_map/ppermute | solution.py:23
  410.2 10.3 %collective-permute-start.63 = (f32[8,8,8,1]{3,0,2,1:T(8,128)S(1)}, f32[8,8,8,1]{3,0,2,1:T(8,128)S(1)}, u32[]{:S(2)}, u32[]{:S(2)}) collective-permute-start(f32[8,8,8,1]{3,0,2,1:T(8,128)S(1)} %get-tuple-element.275), channel_id=1, source_target_pairs={{0,1},{1,2},{2,3},{4,5},{5,6},{6,7},{8,9},{9,10},{10,11},{12,13},{... | collective-permute-start | bytes 6152 | tf_op jit(solution)/shard_map/ppermute | solution.py:21
  412.2 8.3 %collective-permute-start.62 = (f32[8,8,8,1]{3,0,2,1:T(8,128)S(1)}, f32[8,8,8,1]{3,0,2,1:T(8,128)S(1)}, u32[]{:S(2)}, u32[]{:S(2)}) collective-permute-start(f32[8,8,8,1]{3,0,2,1:T(8,128)S(1)} %get-tuple-element.274), channel_id=1, source_target_pairs={{1,0},{2,1},{3,2},{5,4},{6,5},{7,6},{9,8},{10,9},{11,10},{13,12},{... | collective-permute-start | bytes 6152 | tf_op jit(solution)/shard_map/ppermute | solution.py:23
  425.6 9.8 %collective-permute-start.67 = (f32[8,8,8,1]{3,0,2,1:T(8,128)S(1)}, f32[8,8,8,1]{3,0,2,1:T(8,128)S(1)}, u32[]{:S(2)}, u32[]{:S(2)}) collective-permute-start(f32[8,8,8,1]{3,0,2,1:T(8,128)S(1)} %get-tuple-element.267), channel_id=1, source_target_pairs={{0,1},{1,2},{2,3},{4,5},{5,6},{6,7},{8,9},{9,10},{10,11},{12,13},{... | collective-permute-start | bytes 6152 | tf_op jit(solution)/shard_map/ppermute | solution.py:21
  427.6 7.8 %collective-permute-start.66 = (f32[8,8,8,1]{3,0,2,1:T(8,128)S(1)}, f32[8,8,8,1]{3,0,2,1:T(8,128)S(1)}, u32[]{:S(2)}, u32[]{:S(2)}) collective-permute-start(f32[8,8,8,1]{3,0,2,1:T(8,128)S(1)} %get-tuple-element.266), channel_id=1, source_target_pairs={{1,0},{2,1},{3,2},{5,4},{6,5},{7,6},{9,8},{10,9},{11,10},{13,12},{... | collective-permute-start | bytes 6152 | tf_op jit(solution)/shard_map/ppermute | solution.py:23
  502.5 8.2 %collective-permute-start.71 = (f32[8,8,8,1]{3,0,2,1:T(8,128)S(1)}, f32[8,8,8,1]{3,0,2,1:T(8,128)S(1)}, u32[]{:S(2)}, u32[]{:S(2)}) collective-permute-start(f32[8,8,8,1]{3,0,2,1:T(8,128)S(1)} %get-tuple-element.259), channel_id=1, source_target_pairs={{0,1},{1,2},{2,3},{4,5},{5,6},{6,7},{8,9},{9,10},{10,11},{12,13},{... | collective-permute-start | bytes 6152 | tf_op jit(solution)/shard_map/ppermute | solution.py:21
  504.4 7.5 %collective-permute-start.70 = (f32[8,8,8,1]{3,0,2,1:T(8,128)S(1)}, f32[8,8,8,1]{3,0,2,1:T(8,128)S(1)}, u32[]{:S(2)}, u32[]{:S(2)}) collective-permute-start(f32[8,8,8,1]{3,0,2,1:T(8,128)S(1)} %get-tuple-element.258), channel_id=1, source_target_pairs={{1,0},{2,1},{3,2},{5,4},{6,5},{7,6},{9,8},{10,9},{11,10},{13,12},{... | collective-permute-start | bytes 6152 | tf_op jit(solution)/shard_map/ppermute | solution.py:23
  515.9 10.5 %collective-permute-start.75 = (f32[8,8,8,1]{3,0,2,1:T(8,128)S(1)}, f32[8,8,8,1]{3,0,2,1:T(8,128)S(1)}, u32[]{:S(2)}, u32[]{:S(2)}) collective-permute-start(f32[8,8,8,1]{3,0,2,1:T(8,128)S(1)} %get-tuple-element.251), channel_id=1, source_target_pairs={{0,1},{1,2},{2,3},{4,5},{5,6},{6,7},{8,9},{9,10},{10,11},{12,13},{... | collective-permute-start | bytes 6152 | tf_op jit(solution)/shard_map/ppermute | solution.py:21
  517.8 8.6 %collective-permute-start.74 = (f32[8,8,8,1]{3,0,2,1:T(8,128)S(1)}, f32[8,8,8,1]{3,0,2,1:T(8,128)S(1)}, u32[]{:S(2)}, u32[]{:S(2)}) collective-permute-start(f32[8,8,8,1]{3,0,2,1:T(8,128)S(1)} %get-tuple-element.250), channel_id=1, source_target_pairs={{1,0},{2,1},{3,2},{5,4},{6,5},{7,6},{9,8},{10,9},{11,10},{13,12},{... | collective-permute-start | bytes 6152 | tf_op jit(solution)/shard_map/ppermute | solution.py:23
  531.5 9.8 %collective-permute-start.79 = (f32[8,8,8,1]{3,0,2,1:T(8,128)S(1)}, f32[8,8,8,1]{3,0,2,1:T(8,128)S(1)}, u32[]{:S(2)}, u32[]{:S(2)}) collective-permute-start(f32[8,8,8,1]{3,0,2,1:T(8,128)S(1)} %get-tuple-element.243), channel_id=1, source_target_pairs={{0,1},{1,2},{2,3},{4,5},{5,6},{6,7},{8,9},{9,10},{10,11},{12,13},{... | collective-permute-start | bytes 6152 | tf_op jit(solution)/shard_map/ppermute | solution.py:21
  533.4 7.8 %collective-permute-start.78 = (f32[8,8,8,1]{3,0,2,1:T(8,128)S(1)}, f32[8,8,8,1]{3,0,2,1:T(8,128)S(1)}, u32[]{:S(2)}, u32[]{:S(2)}) collective-permute-start(f32[8,8,8,1]{3,0,2,1:T(8,128)S(1)} %get-tuple-element.242), channel_id=1, source_target_pairs={{1,0},{2,1},{3,2},{5,4},{6,5},{7,6},{9,8},{10,9},{11,10},{13,12},{... | collective-permute-start | bytes 6152 | tf_op jit(solution)/shard_map/ppermute | solution.py:23
  546.4 10.5 %collective-permute-start.83 = (f32[8,8,8,1]{3,0,2,1:T(8,128)S(1)}, f32[8,8,8,1]{3,0,2,1:T(8,128)S(1)}, u32[]{:S(2)}, u32[]{:S(2)}) collective-permute-start(f32[8,8,8,1]{3,0,2,1:T(8,128)S(1)} %get-tuple-element.235), channel_id=1, source_target_pairs={{0,1},{1,2},{2,3},{4,5},{5,6},{6,7},{8,9},{9,10},{10,11},{12,13},{... | collective-permute-start | bytes 6152 | tf_op jit(solution)/shard_map/ppermute | solution.py:21
  548.3 8.6 %collective-permute-start.82 = (f32[8,8,8,1]{3,0,2,1:T(8,128)S(1)}, f32[8,8,8,1]{3,0,2,1:T(8,128)S(1)}, u32[]{:S(2)}, u32[]{:S(2)}) collective-permute-start(f32[8,8,8,1]{3,0,2,1:T(8,128)S(1)} %get-tuple-element.234), channel_id=1, source_target_pairs={{1,0},{2,1},{3,2},{5,4},{6,5},{7,6},{9,8},{10,9},{11,10},{13,12},{... | collective-permute-start | bytes 6152 | tf_op jit(solution)/shard_map/ppermute | solution.py:23
  (41 other events, 220.4 us)
